TPU v7x, 32 devices: a whole 2x2x4 slice. The times are simulated.
32 devices in a mesh: sub: 8 (over z, x), tile: 4 (over y, core).
Axes of the slice: x: 2, y: 2, z: 4, core: 2. Of those that a mesh axis runs over, the one named last changes fastest.
Arguments:
- coupling: bfloat16 [8, 28, 256, 256], P('sub'), may hold values from -0.125 to 0.125
- panel_inv: float32 [8, 8, 256, 256], P('sub')
- a_ib: bfloat16 [8, 2048, 3072], P('sub', None, 'tile'), may hold values from -0.5 to 0.5
- owner: int32 [8, 12, 12], P('sub', None, 'tile'), may hold values from 0 to 7, as said below
- slot: int32 [8, 12, 12], P('sub', None, 'tile'), may hold values from 0 to 15
- base: bfloat16 [8, 64, 256, 256], P('sub', 'tile'), may hold values from -2 to 2
Outputs:
- assembled: bfloat16 [8, 64, 256, 256], P('sub', 'tile')
Inputs may be any that keep to these rules, and one draw needn't show every extreme that they name: `owner`: tiles of one device are those of one subdomain s and tile columns t*12/4 to (t+1)*12/4 - 1. At most 5 tiles of one device name one sub index; for each t one sub index, drawn from the seed, is named by exactly 5 tiles of every device of that t.
All inputs are finite; a program needn't handle non-finite values.
Results may differ from a plain program's by a relative error of at most 0.0051.
Values may be sent and summed in bfloat16 or wider, within the bound.
A program may use at most 128 MiB of HBM per device.

v0:
```python
import functools

import jax
import jax.numpy as jnp
from jax import lax
from jax.experimental import pallas as pl
from jax.experimental.pallas import tpu as pltpu
from jax.sharding import PartitionSpec as P

MESH = pl.DeviceIdType.MESH
F32 = jnp.float32
BF16 = jnp.bfloat16


def exchange_kernel(
    dims,
    meta_sm,
    meta_any,
    coupling_hbm,
    inverse_hbm,
    cols_hbm,
    incoming,
    metas,
    labels,
    coupling,
    inverse,
    cols,
    target,
    held,
    total,
    packed,
    table,
    meta_all,
    load_sem,
    own_send,
    own_recv,
    relay_send,
    relay_recv,
    out_send,
    out_recv,
    meta_send,
    meta_recv,
    local_sem,
):
    n_sub, n_tile, panels, width, col_tiles, tile_count, capacity, slots = dims
    me = lax.axis_index("sub")
    col = lax.axis_index("tile")
    half_tile = n_tile // 2
    partner = col + 1 - 2 * (col % 2)
    across = (col + half_tile) % n_tile
    corner = (partner + half_tile) % n_tile
    places = (col, partner, across, corner)
    half = n_sub // 2
    side = me // half
    within = me % half

    def far_peer(j):
        return ((side + 1) % 2) * half + (within + j) % half

    def near_peer(j):
        return side * half + (within + j) % half

    loads = [
        pltpu.make_async_copy(cols_hbm.at[0], cols.at[0], load_sem.at[0]),
        pltpu.make_async_copy(inverse_hbm.at[0], inverse.at[0], load_sem.at[1]),
        pltpu.make_async_copy(coupling_hbm, coupling, load_sem.at[2]),
        pltpu.make_async_copy(
            inverse_hbm.at[pl.ds(1, panels - 1)], inverse.at[pl.ds(1, panels - 1)], load_sem.at[3]
        ),
        pltpu.make_async_copy(
            cols_hbm.at[pl.ds(1, panels - 1)], cols.at[pl.ds(1, panels - 1)], load_sem.at[4]
        ),
    ]
    for load in loads:
        load.start()

    barrier = pltpu.get_barrier_semaphore()
    for place in (partner, across):
        pl.semaphore_signal(barrier, inc=1, device_id={"tile": place}, device_id_type=MESH)

    @pl.loop(1, n_sub)
    def _(j):
        pl.semaphore_signal(
            barrier, inc=1, device_id={"sub": (me + j) % n_sub}, device_id_type=MESH
        )

    def solve_panel(k):
        target[...] = cols[k].astype(F32)
        start = k * (k - 1) // 2
        for m in range(k):
            target[...] -= jnp.dot(coupling[start + m], held[m], preferred_element_type=F32)
        inv = inverse[k]
        inv_high = inv.astype(BF16)
        inv_low = (inv - inv_high.astype(F32)).astype(BF16)
        value = target[...]
        high = value.astype(BF16)
        low = (value - high.astype(F32)).astype(BF16)
        answer = jnp.dot(inv_high, low, preferred_element_type=F32)
        answer += jnp.dot(inv_low, high, preferred_element_type=F32)
        answer += jnp.dot(inv_high, high, preferred_element_type=F32)
        held[k] = answer.astype(BF16)

    def own_copy(k, way):
        return pltpu.make_async_remote_copy(
            src_ref=held.at[k],
            dst_ref=held.at[(way + 1) * panels + k],
            send_sem=own_send.at[way, k],
            recv_sem=own_recv.at[way, k],
            device_id={"tile": (partner, across)[way]},
            device_id_type=MESH,
        )

    def relay_copy(k):
        return pltpu.make_async_remote_copy(
            src_ref=held.at[2 * panels + k],
            dst_ref=held.at[3 * panels + k],
            send_sem=relay_send.at[k],
            recv_sem=relay_recv.at[k],
            device_id={"tile": partner},
            device_id_type=MESH,
        )

    def out_copy(peer, source):
        return pltpu.make_async_remote_copy(
            src_ref=packed.at[peer],
            dst_ref=incoming.at[source],
            send_sem=out_send.at[peer],
            recv_sem=out_recv.at[source],
            device_id={"sub": peer},
            device_id_type=MESH,
        )

    def meta_copy(peer, source):
        return pltpu.make_async_remote_copy(
            src_ref=meta_any,
            dst_ref=metas.at[source],
            send_sem=meta_send.at[peer],
            recv_sem=meta_recv.at[source],
            device_id={"sub": peer},
            device_id_type=MESH,
        )

    loads[0].wait()
    loads[1].wait()
    solve_panel(0)
    pl.semaphore_wait(barrier, n_sub + 1)
    own_copy(0, 1).start()
    own_copy(0, 0).start()
    for load in loads[2:]:
        load.wait()
    for k in range(1, panels):
        solve_panel(k)
        own_copy(k, 1).start()
        own_copy(k, 0).start()

    @pl.loop(1, n_sub)
    def _(j):
        meta_copy((me + j) % n_sub, me).start()

    per_place = col_tiles * col_tiles

    def gram(u, k, first=False):
        right = held[k]
        for i in range(col_tiles):
            left = held[u * panels + k, :, i * width : (i + 1) * width]
            product = lax.dot_general(
                left, right, (((0,), (0,)), ((), ())), preferred_element_type=F32
            )
            for j in range(col_tiles):
                piece = product[:, j * width : (j + 1) * width]
                at = places[u] * per_place + i * col_tiles + j
                if first:
                    total[at] = piece
                else:
                    total[at] += piece

    def pick(read, low, default, value_of, store):
        def body(i, carry):
            count, chosen = carry
            value = read(i)
            hit = (value >= low) & (value < low + slots)
            new = value_of(i, value)
            chosen = tuple(
                jnp.where(hit & (count == r), new, c) for r, c in enumerate(chosen)
            )
            return count + jnp.where(hit, 1, 0), chosen

        start = (jnp.int32(0), tuple(jnp.int32(default) for _ in range(capacity)))
        _, chosen = lax.fori_loop(0, tile_count, body, start)
        for r, c in enumerate(chosen):
            store(r, c)

    @pl.loop(0, n_sub)
    def _(d):
        def store(r, c):
            table[d * capacity + r] = c

        pick(lambda i: meta_sm[0, i], d * slots, 0, lambda i, v: i, store)

    gram(0, 0, first=True)

    @pl.loop(1, panels)
    def _(k):
        gram(0, k)

    own_copy(0, 0).wait_recv()
    gram(1, 0, first=True)

    @pl.loop(1, panels)
    def _(k):
        own_copy(k, 0).wait_recv()
        gram(1, k)

    def remote_step(k, first):
        own_copy(k, 1).wait_recv()
        relay_copy(k).start()
        gram(2, k, first)
        relay_copy(k).wait_recv()
        gram(3, k, first)

    remote_step(0, True)

    @pl.loop(1, panels)
    def _(k):
        remote_step(k, False)

    def pack(d):
        for r in range(capacity):
            packed[d, r] = (-total[table[d * capacity + r]]).astype(BF16)

    @pl.loop(0, half)
    def _(j):
        pack(far_peer(j))
        out_copy(far_peer(j), me).start()

    @pl.loop(1, half)
    def _(j):
        pack(near_peer(j))
        out_copy(near_peer(j), me).start()

    pack(me)
    keep = pltpu.make_async_copy(packed.at[me], incoming.at[me], local_sem.at[0])
    keep.start()

    own_meta = pltpu.make_async_copy(meta_any, meta_all.at[me], local_sem.at[1])
    own_meta.start()

    @pl.loop(1, n_sub)
    def _(j):
        source = (me + j) % n_sub
        meta_copy(source, source).wait_recv()
        fetch = pltpu.make_async_copy(metas.at[source], meta_all.at[source], local_sem.at[2])
        fetch.start()
        fetch.wait()

    own_meta.wait()

    @pl.loop(0, n_sub)
    def _(s):
        def store(r, c):
            labels[s * capacity + r] = c

        pick(
            lambda i: meta_all[s, 0, i], me * slots, slots, lambda i, v: v - me * slots, store
        )

    @pl.loop(0, panels)
    def _(k):
        own_copy(k, 0).wait_send()
        own_copy(k, 1).wait_send()
        relay_copy(k).wait_send()

    @pl.loop(1, n_sub)
    def _(j):
        source = (me + j) % n_sub
        meta_copy(source, source).wait_send()
        out_copy(source, source).wait_send()
        out_copy(source, source).wait_recv()

    keep.wait()


def add_kernel(slots, capacity, labels, incoming, base, result, total):
    step = pl.program_id(0)

    @pl.when(step == 0)
    def _():
        total[pl.ds(0, slots)] = base[...].astype(F32)

    for r in range(capacity):
        total[labels[step * capacity + r]] += incoming[0, r].astype(F32)

    @pl.when(step == pl.num_programs(0) - 1)
    def _():
        result[...] = total[pl.ds(0, slots)].astype(BF16)


def shards(coupling, panel_inv, a_ib, owner, slot, base):
    lower_blocks = coupling[0]
    inverse = panel_inv[0]
    panels, width = inverse.shape[:2]
    col_count = a_ib.shape[2]
    right_cols = a_ib[0].reshape(panels, width, col_count)
    n_sub = lax.axis_size("sub")
    n_tile = lax.axis_size("tile")
    assert n_tile == 4 and n_sub % 2 == 0
    col_tiles = col_count // width
    tile_count = owner.shape[1] * owner.shape[2]
    assert owner.shape[1] == n_tile * col_tiles
    capacity = (tile_count + n_sub - 1) // n_sub
    slots = base.shape[1]
    room = (tile_count + 127) // 128 * 128
    meta = (owner[0] * slots + slot[0]).reshape(1, tile_count)
    meta = jnp.pad(meta, ((0, 0), (0, room - tile_count)))
    dims = (n_sub, n_tile, panels, width, col_tiles, tile_count, capacity, slots)
    any_spec = pl.BlockSpec(memory_space=pl.ANY)
    smem_spec = pl.BlockSpec(memory_space=pltpu.SMEM)
    dma = pltpu.SemaphoreType.DMA
    incoming, _, labels = pl.pallas_call(
        functools.partial(exchange_kernel, dims),
        out_shape=(
            jax.ShapeDtypeStruct((n_sub, capacity, width, width), BF16),
            jax.ShapeDtypeStruct((n_sub, 1, room), jnp.int32),
            jax.ShapeDtypeStruct((n_sub * capacity,), jnp.int32),
        ),
        in_specs=[smem_spec, any_spec, any_spec, any_spec, any_spec],
        out_specs=(any_spec, any_spec, smem_spec),
        scratch_shapes=[
            pltpu.VMEM(lower_blocks.shape, BF16),
            pltpu.VMEM(inverse.shape, F32),
            pltpu.VMEM(right_cols.shape, BF16),
            pltpu.VMEM((width, col_count), F32),
            pltpu.VMEM((n_tile * panels, width, col_count), BF16),
            pltpu.VMEM((tile_count, width, width), F32),
            pltpu.VMEM((n_sub, capacity, width, width), BF16),
            pltpu.SMEM((n_sub * capacity,), jnp.int32),
            pltpu.SMEM((n_sub, 1, room), jnp.int32),
            dma((5,)),
            dma((2, panels)),
            dma((2, panels)),
            dma((panels,)),
            dma((panels,)),
            dma((n_sub,)),
            dma((n_sub,)),
            dma((n_sub,)),
            dma((n_sub,)),
            dma((3,)),
        ],
        compiler_params=pltpu.CompilerParams(
            collective_id=0, has_side_effects=True, vmem_limit_bytes=60 * 1024 * 1024
        ),
    )(meta, meta, lower_blocks, inverse, right_cols)

    whole_block = pl.BlockSpec((slots, width, width), lambda s: (0, 0, 0))
    result = pl.pallas_call(
        functools.partial(add_kernel, slots, capacity),
        grid=(n_sub,),
        out_shape=jax.ShapeDtypeStruct((slots, width, width), BF16),
        in_specs=[
            smem_spec,
            pl.BlockSpec((1, capacity, width, width), lambda s: (s, 0, 0, 0)),
            whole_block,
        ],
        out_specs=whole_block,
        scratch_shapes=[pltpu.VMEM((slots + 1, width, width), F32)],
        compiler_params=pltpu.CompilerParams(vmem_limit_bytes=32 * 1024 * 1024),
    )(labels, incoming, base[0])
    return result[None]


def solution(mesh):
    placed = (
        P("sub", None, None, None),
        P("sub", None, None, None),
        P("sub", None, "tile"),
        P("sub", None, "tile"),
        P("sub", None, "tile"),
        P("sub", "tile", None, None),
    )
    return jax.shard_map(
        shards, mesh=mesh, in_specs=placed, out_specs=P("sub", "tile", None, None), check_vma=False
    )
```

profile of v0, /device:TPU:0, one launch (start us, length us, event | category | flops | bytes accessed | tf_op | source)
XLA Modules:
  0.0 202.1 jit_solution(15653830999405506191)
XLA Ops:
  0.0 0.7 multiply_add_fusion
  0.7 0.1 copy.8
  0.8 0.1 add.16
  0.9 0.5 pad.4.meta_sm.meta_any
  1.4 0.0 copy-start.1
  1.4 194.1 %shard_map.64 = (bf16[8,5,256,256]{3,2,1,0:T(8,128)(2,1)}, s32[8,1,128]{2,1,0:T(1,128)}, s32[40]{0:T(128)}) custom-call(s32[1,128]{1,0:T(1,128)} %pad.4.meta_sm.meta_any, s32[1,128]{1,0:T(1,128)} %pad.4.meta_sm.meta_any, bf16[28,256,256]{2,1,0:T(8,128)(2,1)} %bitcast.6, f32[8,256,256]{2,1,0:T(8,128)} %bitcast.8, bf16[8,256,768]{2,1,0:T(8,128)(2,1)} %bitcast.7), custom_call_target="tpu_custom_call" | custom-call | tf_op jit(solution)/shard_map/pallas_call | solution.py:319
  195.5 0.0 copy-done.1
  195.5 0.0 copy-start
  195.5 2.5 %copy-done = bf16[8,5,256,256]{3,2,1,0:T(8,128)(2,1)S(1)} copy-done((bf16[8,5,256,256]{3,2,1,0:T(8,128)(2,1)S(1)}, bf16[8,5,256,256]{3,2,1,0:T(8,128)(2,1)}, u32[]{:S(2)}) %copy-start) | copy-done | bytes 5242904
  198.0 0.0 copy-start.2
  198.0 0.6 copy-done.2
  198.6 3.5 %shard_map.65 = bf16[16,256,256]{2,1,0:T(8,128)(2,1)} custom-call(s32[40]{0:T(128)S(1)} %copy-done.2, bf16[8,5,256,256]{3,2,1,0:T(8,128)(2,1)S(1)} %copy-done, bf16[16,256,256]{2,1,0:T(8,128)(2,1)S(1)} %bitcast.5), custom_call_target="tpu_custom_call" | custom-call | tf_op jit(solution)/shard_map/pallas_call | solution.py:355
Async XLA Ops:
  1.4 194.1 %copy-start.1 = (bf16[1,16,256,256]{3,2,1,0:T(8,128)(2,1)S(1)}, bf16[1,16,256,256]{3,2,1,0:T(8,128)(2,1)}, u32[]{:S(2)}) copy-start(bf16[1,16,256,256]{3,2,1,0:T(8,128)(2,1)} %param.11) | copy-start | bytes 6291460
  195.5 2.5 %copy-start = (bf16[8,5,256,256]{3,2,1,0:T(8,128)(2,1)S(1)}, bf16[8,5,256,256]{3,2,1,0:T(8,128)(2,1)}, u32[]{:S(2)}) copy-start(bf16[8,5,256,256]{3,2,1,0:T(8,128)(2,1)} %get-tuple-element.8.incoming) | copy-start | bytes 15728644
  198.0 0.6 copy-start.2
where the time goes:
time: 202 us
  Pallas kernels  198 us (98%)
  local copies, waits for them, and re-layouts  3.79 us (2%)
    pallas_call x1, Pallas kernels, shards(): pl.pallas_call(functools.partial(exchange_kernel, dims), out_shape=(jax.S...  194 us

commit v1 on v0

v1 whole, which is shorter than its diff:
```python
import functools

import jax
import jax.numpy as jnp
from jax import lax
from jax.experimental import pallas as pl
from jax.experimental.pallas import tpu as pltpu
from jax.sharding import PartitionSpec as P

MESH = pl.DeviceIdType.MESH
F32 = jnp.float32
BF16 = jnp.bfloat16
GROUP = 8


def flip(value, bit, on):
    return value + on * (bit - 2 * bit * ((value // bit) % 2))


def flip_mask(value, mask):
    for bit in (1, 2, 4):
        value = flip(value, bit, (mask // bit) % 2)
    return value


def inner_order(i):
    high = i // 4
    first = 5 - 2 * (i % 2) - i // 2
    last = 7 - (i - 4) - 4 * ((i - 4) // 2)
    return (1 - high) * first + high * last


def kernel(
    dims,
    meta_sm,
    meta_any,
    coupling_hbm,
    inverse_hbm,
    cols_hbm,
    base_hbm,
    result,
    metas,
    coupling,
    inverse,
    cols,
    base,
    held,
    detour,
    packed,
    incoming,
    total,
    table,
    labels,
    meta_all,
    load_sem,
    own_send,
    own_recv,
    relay_send,
    relay_recv,
    detour_send,
    detour_recv,
    forward_send,
    forward_recv,
    out_send,
    out_recv,
    meta_send,
    meta_recv,
    local_sem,
):
    n_sub, n_tile, panels, width, col_tiles, tile_count, capacity, slots = dims
    me = lax.axis_index("sub")
    col = lax.axis_index("tile")
    rows = tile_count // col_tiles
    half_tile = n_tile // 2
    partner = col + 1 - 2 * (col % 2)
    across = (col + half_tile) % n_tile
    groups = n_sub // GROUP
    group = me // GROUP
    within = me % GROUP
    inner = ((within // 2 + 1) % 4) // 2
    mate = flip(me, 2, 1)
    detoured = [k for k in range(panels) if k % 2 == 1][: panels * 3 // 8]
    direct = [k for k in range(panels) if k not in detoured]

    def send_mask(step):
        place = step % GROUP
        return inner * inner_order(place) + (1 - inner) * (GROUP - 1 - place)

    def send_peer(step):
        mask = send_mask(step)
        return ((group + 1 + step // GROUP) % groups) * GROUP + flip_mask(within, mask)

    def slot_at(step, peer, mask):
        role = ((peer % GROUP // 2 + 1) % 4) // 2
        some = (mask + GROUP - 1) // GROUP
        at = (8 + 4 * role - mask) % (GROUP - 1)
        return step // GROUP * GROUP + some * at + (1 - some) * (GROUP - 1)

    def source_peer(step):
        place = step % GROUP
        some = 1 - place // (GROUP - 1)
        mask = some * ((7 + 4 * inner - place) % (GROUP - 1) + 1)
        return ((group + 2 * groups - 1 - step // GROUP) % groups) * GROUP + flip_mask(within, mask)

    loads = [
        pltpu.make_async_copy(cols_hbm.at[0], cols.at[0], load_sem.at[0]),
        pltpu.make_async_copy(inverse_hbm.at[0], inverse.at[0], load_sem.at[1]),
        pltpu.make_async_copy(coupling_hbm, coupling, load_sem.at[2]),
        pltpu.make_async_copy(
            inverse_hbm.at[pl.ds(1, panels - 1)], inverse.at[pl.ds(1, panels - 1)], load_sem.at[3]
        ),
        pltpu.make_async_copy(
            cols_hbm.at[pl.ds(1, panels - 1)], cols.at[pl.ds(1, panels - 1)], load_sem.at[4]
        ),
    ]
    for load in loads:
        load.start()
    base_load = pltpu.make_async_copy(base_hbm, base, load_sem.at[5])
    base_load.start()

    barrier = pltpu.get_barrier_semaphore()
    for place in (partner, across):
        pl.semaphore_signal(barrier, inc=1, device_id={"tile": place}, device_id_type=MESH)
    pl.semaphore_signal(
        barrier, inc=1, device_id={"sub": mate, "tile": across}, device_id_type=MESH
    )

    @pl.loop(1, n_sub)
    def _(j):
        pl.semaphore_signal(
            barrier, inc=1, device_id={"sub": (me + j) % n_sub}, device_id_type=MESH
        )

    def block(where, k):
        return held.at[where * panels + k]

    def solve_panel(k):
        start = k * (k - 1) // 2
        inv = inverse[k]
        inv_high = inv.astype(BF16)
        inv_low = (inv - inv_high.astype(F32)).astype(BF16)
        for i in range(col_tiles):
            value = cols[k, :, i * width : (i + 1) * width].astype(F32)
            if k:
                value -= sum(
                    jnp.dot(
                        coupling[start + m],
                        held[col * panels + m, i],
                        preferred_element_type=F32,
                    )
                    for m in range(k)
                )
            high = value.astype(BF16)
            low = (value - high.astype(F32)).astype(BF16)
            answer = jnp.dot(inv_high, low, preferred_element_type=F32)
            answer += jnp.dot(inv_low, high, preferred_element_type=F32)
            answer += jnp.dot(inv_high, high, preferred_element_type=F32)
            held[col * panels + k, i] = answer.astype(BF16)

    def own_copy(k, way):
        return pltpu.make_async_remote_copy(
            src_ref=block(col, k),
            dst_ref=block(col, k),
            send_sem=own_send.at[way, k],
            recv_sem=own_recv.at[way, k],
            device_id={"tile": (partner, across)[way]},
            device_id_type=MESH,
        )

    def relay_copy(k):
        return pltpu.make_async_remote_copy(
            src_ref=block(across, k),
            dst_ref=block(across, k),
            send_sem=relay_send.at[k],
            recv_sem=relay_recv.at[k],
            device_id={"tile": partner},
            device_id_type=MESH,
        )

    def detour_copy(j):
        return pltpu.make_async_remote_copy(
            src_ref=block(col, detoured[j]),
            dst_ref=detour.at[j],
            send_sem=detour_send.at[j],
            recv_sem=detour_recv.at[j],
            device_id={"sub": mate, "tile": across},
            device_id_type=MESH,
        )

    def forward_copy(j):
        return pltpu.make_async_remote_copy(
            src_ref=detour.at[j],
            dst_ref=block(across, detoured[j]),
            send_sem=forward_send.at[j],
            recv_sem=forward_recv.at[j],
            device_id={"sub": mate},
            device_id_type=MESH,
        )

    def out_copy(step, r, peer, at):
        return pltpu.make_async_remote_copy(
            src_ref=packed.at[step, r],
            dst_ref=incoming.at[at, r],
            send_sem=out_send.at[step, r],
            recv_sem=out_recv.at[at, r],
            device_id={"sub": peer},
            device_id_type=MESH,
        )

    def meta_copy(peer, source):
        return pltpu.make_async_remote_copy(
            src_ref=meta_any,
            dst_ref=metas.at[source],
            send_sem=meta_send.at[peer],
            recv_sem=meta_recv.at[source],
            device_id={"sub": peer},
            device_id_type=MESH,
        )

    def start_panel(k):
        own_copy(k, 0).start()

        @pl.when(inner == 0)
        def _():
            if k in detoured:
                detour_copy(detoured.index(k)).start()
            else:
                own_copy(k, 1).start()

    loads[0].wait()
    loads[1].wait()
    solve_panel(0)
    pl.semaphore_wait(barrier, n_sub + 2)
    start_panel(0)
    for load in loads[2:]:
        load.wait()
    for k in range(1, panels):
        solve_panel(k)
        start_panel(k)

    @pl.loop(1, n_sub)
    def _(j):
        meta_copy((me + j) % n_sub, me).start()

    own_meta = pltpu.make_async_copy(meta_any, meta_all.at[me], local_sem.at[1])
    own_meta.start()

    def pick(read, low, default, value_of, store):
        def body(i, carry):
            count, chosen = carry
            value = read(i)
            hit = (value >= low) & (value < low + slots)
            new = value_of(i, value)
            chosen = tuple(
                jnp.where(hit & (count == r), new, c) for r, c in enumerate(chosen)
            )
            return count + jnp.where(hit, 1, 0), chosen

        start = (jnp.int32(0), tuple(jnp.int32(default) for _ in range(capacity)))
        _, chosen = lax.fori_loop(0, tile_count, body, start)
        for r, c in enumerate(chosen):
            store(r, c)

    @pl.loop(0, n_sub)
    def _(d):
        def store(r, c):
            table[d * capacity + r] = c

        pick(lambda i: meta_sm[0, i], d * slots, 0, lambda i, v: i, store)

    @pl.when(inner == 1)
    def _():
        for j in range(len(detoured)):
            detour_copy(j).wait_recv()
            forward_copy(j).start()
        for k in range(panels):
            own_copy(k, 1).start()

    @pl.loop(1, n_sub)
    def _(j):
        source = (me + j) % n_sub
        meta_copy(source, source).wait_recv()
        fetch = pltpu.make_async_copy(metas.at[source], meta_all.at[source], local_sem.at[2])
        fetch.start()
        fetch.wait()

    own_meta.wait()

    @pl.loop(0, n_sub)
    def _(s):
        def store(r, c):
            labels[s * capacity + r] = c

        pick(
            lambda i: meta_all[s, 0, i], me * slots, slots, lambda i, v: v - me * slots, store
        )

    base_load.wait()

    @pl.loop(0, slots)
    def _(q):
        total[q] = base[q].astype(F32)

    @pl.when(inner == 0)
    def _():
        for k in sorted(range(panels), key=lambda k: k + (1.5 if k in detoured else 0)):
            if k in detoured:
                forward_copy(detoured.index(k)).wait_recv()
            else:
                own_copy(k, 1).wait_recv()
            relay_copy(k).start()

    @pl.when(inner == 1)
    def _():
        for k in range(panels):
            own_copy(k, 1).wait_recv()
            relay_copy(k).start()

    for k in range(panels):
        own_copy(k, 0).wait_recv()
        relay_copy(k).wait_recv()

    def tile_of(entry):
        right = entry // rows
        left = entry % rows
        place = left // col_tiles
        product = sum(
            lax.dot_general(
                held[place * panels + k, left % col_tiles],
                held[col * panels + k, right],
                (((0,), (0,)), ((), ())),
                preferred_element_type=F32,
            )
            for k in range(panels)
        )
        return (-product).astype(BF16)

    @pl.loop(0, n_sub - 1)
    def _(step):
        peer = send_peer(step)
        for r in range(capacity):
            packed[step, r] = tile_of(table[peer * capacity + r])
            out_copy(step, r, peer, slot_at(step, peer, send_mask(step))).start()

    for r in range(capacity):
        packed[n_sub - 1, r] = tile_of(table[me * capacity + r])

    strip = 32

    def gather(tiles, source):
        wanted = [labels[source * capacity + r] for r in range(capacity)]
        for c in range(width // strip):
            at = slice(c * strip, (c + 1) * strip)
            parts = [tiles(r, at).astype(F32) for r in range(capacity)]

            @pl.loop(0, slots)
            def _(q):
                value = total[q, at]
                for r in range(capacity):
                    value += jnp.where(wanted[r] == q, parts[r], 0.0)
                total[q, at] = value

    gather(lambda r, at: packed[n_sub - 1, r, at], me)

    @pl.loop(0, n_sub - 1)
    def _(step):
        source = source_peer(step)
        for r in range(capacity):
            out_copy(step, r, source, step).wait_recv()
        gather(lambda r, at: incoming[step, r, at], source)

    @pl.loop(0, slots)
    def _(q):
        result[q] = total[q].astype(BF16)

    for k in range(panels):
        own_copy(k, 0).wait_send()
        relay_copy(k).wait_send()

    @pl.when(inner == 0)
    def _():
        for k in direct:
            own_copy(k, 1).wait_send()
        for j in range(len(detoured)):
            detour_copy(j).wait_send()

    @pl.when(inner == 1)
    def _():
        for k in range(panels):
            own_copy(k, 1).wait_send()
        for j in range(len(detoured)):
            forward_copy(j).wait_send()

    @pl.loop(1, n_sub)
    def _(j):
        source = (me + j) % n_sub
        meta_copy(source, source).wait_send()

    @pl.loop(0, n_sub - 1)
    def _(step):
        for r in range(capacity):
            out_copy(step, r, me, step).wait_send()


def shards(coupling, panel_inv, a_ib, owner, slot, base):
    lower_blocks = coupling[0]
    inverse = panel_inv[0]
    panels, width = inverse.shape[:2]
    col_count = a_ib.shape[2]
    right_cols = a_ib[0].reshape(panels, width, col_count)
    n_sub = lax.axis_size("sub")
    n_tile = lax.axis_size("tile")
    assert n_tile == 4 and n_sub % GROUP == 0
    col_tiles = col_count // width
    tile_count = owner.shape[1] * owner.shape[2]
    assert owner.shape[1] == n_tile * col_tiles
    capacity = (tile_count + n_sub - 1) // n_sub
    slots = base.shape[1]
    room = (tile_count + 127) // 128 * 128
    meta = (owner[0] * slots + slot[0]).T.reshape(1, tile_count)
    meta = jnp.pad(meta, ((0, 0), (0, room - tile_count)))
    dims = (n_sub, n_tile, panels, width, col_tiles, tile_count, capacity, slots)
    relayed = panels * 3 // 8
    any_spec = pl.BlockSpec(memory_space=pl.ANY)
    smem_spec = pl.BlockSpec(memory_space=pltpu.SMEM)
    dma = pltpu.SemaphoreType.DMA
    result, _ = pl.pallas_call(
        functools.partial(kernel, dims),
        out_shape=(
            jax.ShapeDtypeStruct((slots, width, width), BF16),
            jax.ShapeDtypeStruct((n_sub, 1, room), jnp.int32),
        ),
        in_specs=[smem_spec, any_spec, any_spec, any_spec, any_spec, any_spec],
        out_specs=(pl.BlockSpec(memory_space=pltpu.VMEM), any_spec),
        scratch_shapes=[
            pltpu.VMEM(lower_blocks.shape, BF16),
            pltpu.VMEM(inverse.shape, F32),
            pltpu.VMEM(right_cols.shape, BF16),
            pltpu.VMEM((slots, width, width), BF16),
            pltpu.VMEM((n_tile * panels, col_tiles, width, width), BF16),
            pltpu.VMEM((relayed, col_tiles, width, width), BF16),
            pltpu.VMEM((n_sub, capacity, width, width), BF16),
            pltpu.VMEM((n_sub - 1, capacity, width, width), BF16),
            pltpu.VMEM((slots, width, width), F32),
            pltpu.SMEM((n_sub * capacity,), jnp.int32),
            pltpu.SMEM((n_sub * capacity,), jnp.int32),
            pltpu.SMEM((n_sub, 1, room), jnp.int32),
            dma((6,)),
            dma((2, panels)),
            dma((2, panels)),
            dma((panels,)),
            dma((panels,)),
            dma((relayed,)),
            dma((relayed,)),
            dma((relayed,)),
            dma((relayed,)),
            dma((n_sub, capacity)),
            dma((n_sub, capacity)),
            dma((n_sub,)),
            dma((n_sub,)),
            dma((3,)),
        ],
        compiler_params=pltpu.CompilerParams(
            collective_id=0, has_side_effects=True, vmem_limit_bytes=62 * 1024 * 1024
        ),
    )(meta, meta, lower_blocks, inverse, right_cols, base[0])
    return result[None]


def solution(mesh):
    placed = (
        P("sub", None, None, None),
        P("sub", None, None, None),
        P("sub", None, "tile"),
        P("sub", None, "tile"),
        P("sub", None, "tile"),
        P("sub", "tile", None, None),
    )
    return jax.shard_map(
        shards, mesh=mesh, in_specs=placed, out_specs=P("sub", "tile", None, None), check_vma=False
    )
```

time: 202 us -> 175 us (0.87)
  Pallas kernels: 198 us -> 170 us
    pallas_call x2 -> x1, Pallas kernels: 198 us -> 170 us  [shards(): pl.pallas_call(functools.partial(kernel, dims), out_shape=(jax.ShapeDtype...]
where the time goes in v1:
time: 175 us
  Pallas kernels  170 us (97%)
  local copies, waits for them, and re-layouts  3.7 us (2%)
    pallas_call x1, Pallas kernels, shards(): pl.pallas_call(functools.partial(kernel, dims), out_shape=(jax.ShapeDtype...  170 us

profile of v1, /device:TPU:0, one launch (start us, length us, event | category | flops | bytes accessed | tf_op | source)
XLA Modules:
  0.0 174.9 jit_solution(9976468386551337)
XLA Ops:
  0.0 0.7 multiply_add_fusion
  0.7 0.1 reshape.6
  0.8 0.5 pad.4.meta_sm.meta_any
  1.3 170.5 %shard_map.64 = (bf16[16,256,256]{2,1,0:T(8,128)(2,1)}, s32[8,1,128]{2,1,0:T(1,128)}) custom-call(s32[1,128]{1,0:T(1,128)} %pad.4.meta_sm.meta_any, s32[1,128]{1,0:T(1,128)} %pad.4.meta_sm.meta_any, bf16[28,256,256]{2,1,0:T(8,128)(2,1)} %bitcast.10, f32[8,256,256]{2,1,0:T(8,128)} %bitcast.13, bf16[8,256,768]{2,1,0:T(8,128)(2,1)} %bitcast.11, ...), custom_call_target="tpu_custom_call" | custom-call | tf_op jit(solution)/shard_map/pallas_call | solution.py:427
  171.8 3.1 %copy.11 = bf16[1,16,256,256]{3,2,1,0:T(8,128)(2,1)} copy(bf16[1,16,256,256]{3,2,1,0:T(8,128)(2,1)} %bitcast.12) | data formatting | bytes 4194304
  (1 shorter events, 0.0 us)

commit v2 on v1

--- a/solution.py
+++ b/solution.py
@@ -28,6 +28,10 @@
     first = 5 - 2 * (i % 2) - i // 2
     last = 7 - (i - 4) - 4 * ((i - 4) // 2)
     return (1 - high) * first + high * last
+
+
+def detour_chunks(chunks):
+    return list(range(1, chunks, 2))[: chunks * 10 // 24]
 
 
 def kernel(
@@ -44,6 +48,7 @@
     inverse,
     cols,
     base,
+    ahead,
     held,
     detour,
     packed,
@@ -53,6 +58,8 @@
     labels,
     meta_all,
     load_sem,
+    near_send,
+    near_recv,
     own_send,
     own_recv,
     relay_send,
@@ -79,8 +86,9 @@
     within = me % GROUP
     inner = ((within // 2 + 1) % 4) // 2
     mate = flip(me, 2, 1)
-    detoured = [k for k in range(panels) if k % 2 == 1][: panels * 3 // 8]
-    direct = [k for k in range(panels) if k not in detoured]
+    chunks = panels * col_tiles
+    detoured = detour_chunks(chunks)
+    direct = [c for c in range(chunks) if c not in detoured]
 
     def send_mask(step):
         place = step % GROUP
@@ -134,52 +142,70 @@
     def block(where, k):
         return held.at[where * panels + k]
 
+    def chunk(where, c):
+        return held.at[where * panels + c // col_tiles, c % col_tiles]
+
+    def update(k, i, value, sources):
+        for m in sources:
+            value -= jnp.dot(
+                coupling[k * (k - 1) // 2 + m], held[col * panels + m, i], preferred_element_type=F32
+            )
+        return value
+
     def solve_panel(k):
-        start = k * (k - 1) // 2
         inv = inverse[k]
         inv_high = inv.astype(BF16)
         inv_low = (inv - inv_high.astype(F32)).astype(BF16)
         for i in range(col_tiles):
-            value = cols[k, :, i * width : (i + 1) * width].astype(F32)
-            if k:
-                value -= sum(
-                    jnp.dot(
-                        coupling[start + m],
-                        held[col * panels + m, i],
-                        preferred_element_type=F32,
-                    )
-                    for m in range(k)
-                )
+            if k > 1:
+                value = ahead[k % 2, i]
+            else:
+                value = cols[k, :, i * width : (i + 1) * width].astype(F32)
+            value = update(k, i, value, range(max(k - 1, 0), k))
             high = value.astype(BF16)
             low = (value - high.astype(F32)).astype(BF16)
             answer = jnp.dot(inv_high, low, preferred_element_type=F32)
             answer += jnp.dot(inv_low, high, preferred_element_type=F32)
             answer += jnp.dot(inv_high, high, preferred_element_type=F32)
             held[col * panels + k, i] = answer.astype(BF16)
-
-    def own_copy(k, way):
+        if 0 < k < panels - 1:
+            for i in range(col_tiles):
+                value = cols[k + 1, :, i * width : (i + 1) * width].astype(F32)
+                ahead[(k + 1) % 2, i] = update(k + 1, i, value, range(k))
+
+    def near_copy(k):
         return pltpu.make_async_remote_copy(
             src_ref=block(col, k),
             dst_ref=block(col, k),
-            send_sem=own_send.at[way, k],
-            recv_sem=own_recv.at[way, k],
-            device_id={"tile": (partner, across)[way]},
-            device_id_type=MESH,
-        )
-
-    def relay_copy(k):
-        return pltpu.make_async_remote_copy(
-            src_ref=block(across, k),
-            dst_ref=block(across, k),
-            send_sem=relay_send.at[k],
-            recv_sem=relay_recv.at[k],
+            send_sem=near_send.at[k],
+            recv_sem=near_recv.at[k],
             device_id={"tile": partner},
             device_id_type=MESH,
         )
 
+    def own_copy(c):
+        return pltpu.make_async_remote_copy(
+            src_ref=chunk(col, c),
+            dst_ref=chunk(col, c),
+            send_sem=own_send.at[c],
+            recv_sem=own_recv.at[c],
+            device_id={"tile": across},
+            device_id_type=MESH,
+        )
+
+    def relay_copy(c):
+        return pltpu.make_async_remote_copy(
+            src_ref=chunk(across, c),
+            dst_ref=chunk(across, c),
+            send_sem=relay_send.at[c],
+            recv_sem=relay_recv.at[c],
+            device_id={"tile": partner},
+            device_id_type=MESH,
+        )
+
     def detour_copy(j):
         return pltpu.make_async_remote_copy(
-            src_ref=block(col, detoured[j]),
+            src_ref=chunk(col, detoured[j]),
             dst_ref=detour.at[j],
             send_sem=detour_send.at[j],
             recv_sem=detour_recv.at[j],
@@ -190,7 +216,7 @@
     def forward_copy(j):
         return pltpu.make_async_remote_copy(
             src_ref=detour.at[j],
-            dst_ref=block(across, detoured[j]),
+            dst_ref=chunk(across, detoured[j]),
             send_sem=forward_send.at[j],
             recv_sem=forward_recv.at[j],
             device_id={"sub": mate},
@@ -218,25 +244,25 @@
         )
 
     def start_panel(k):
-        own_copy(k, 0).start()
-
         @pl.when(inner == 0)
         def _():
-            if k in detoured:
-                detour_copy(detoured.index(k)).start()
-            else:
-                own_copy(k, 1).start()
+            for c in range(k * col_tiles, (k + 1) * col_tiles):
+                if c in detoured:
+                    detour_copy(detoured.index(c)).start()
+                else:
+                    own_copy(c).start()
 
     loads[0].wait()
     loads[1].wait()
-    solve_panel(0)
-    pl.semaphore_wait(barrier, n_sub + 2)
-    start_panel(0)
-    for load in loads[2:]:
-        load.wait()
-    for k in range(1, panels):
+    for k in range(panels):
+        if k == 1:
+            for load in loads[2:]:
+                load.wait()
         solve_panel(k)
+        if k == 0:
+            pl.semaphore_wait(barrier, n_sub + 2)
         start_panel(k)
+        near_copy(k).start()
 
     @pl.loop(1, n_sub)
     def _(j):
@@ -248,33 +274,36 @@
     def pick(read, low, default, value_of, store):
         def body(i, carry):
             count, chosen = carry
-            value = read(i)
-            hit = (value >= low) & (value < low + slots)
-            new = value_of(i, value)
-            chosen = tuple(
-                jnp.where(hit & (count == r), new, c) for r, c in enumerate(chosen)
-            )
-            return count + jnp.where(hit, 1, 0), chosen
+            for j in range(col_tiles):
+                value = read(j, i)
+                hit = (value >= low) & (value < low + slots)
+                new = value_of(j * rows + i, value)
+                chosen = tuple(
+                    jnp.where(hit & (count == r), new, c) for r, c in enumerate(chosen)
+                )
+                count += jnp.where(hit, 1, 0)
+            return count, chosen
 
         start = (jnp.int32(0), tuple(jnp.int32(default) for _ in range(capacity)))
-        _, chosen = lax.fori_loop(0, tile_count, body, start)
+        _, chosen = lax.fori_loop(0, rows, body, start)
         for r, c in enumerate(chosen):
             store(r, c)
-
-    @pl.loop(0, n_sub)
-    def _(d):
-        def store(r, c):
-            table[d * capacity + r] = c
-
-        pick(lambda i: meta_sm[0, i], d * slots, 0, lambda i, v: i, store)
 
     @pl.when(inner == 1)
     def _():
         for j in range(len(detoured)):
             detour_copy(j).wait_recv()
             forward_copy(j).start()
-        for k in range(panels):
-            own_copy(k, 1).start()
+            if j == len(detoured) - 2:
+                for c in range(chunks):
+                    own_copy(c).start()
+
+    @pl.loop(0, n_sub)
+    def _(d):
+        def store(r, c):
+            table[d * capacity + r] = c
+
+        pick(lambda j, i: meta_sm[j, i], d * slots, 0, lambda i, v: i, store)
 
     @pl.loop(1, n_sub)
     def _(j):
@@ -292,7 +321,7 @@
             labels[s * capacity + r] = c
 
         pick(
-            lambda i: meta_all[s, 0, i], me * slots, slots, lambda i, v: v - me * slots, store
+            lambda j, i: meta_all[s, j, i], me * slots, slots, lambda i, v: v - me * slots, store
         )
 
     base_load.wait()
@@ -303,22 +332,25 @@
 
     @pl.when(inner == 0)
     def _():
-        for k in sorted(range(panels), key=lambda k: k + (1.5 if k in detoured else 0)):
-            if k in detoured:
-                forward_copy(detoured.index(k)).wait_recv()
+        arrivals = [(n, c) for n, c in enumerate(direct)]
+        arrivals += [(n + 2.5, c) for n, c in enumerate(detoured)]
+        for _, c in sorted(arrivals):
+            if c in detoured:
+                forward_copy(detoured.index(c)).wait_recv()
             else:
-                own_copy(k, 1).wait_recv()
-            relay_copy(k).start()
+                own_copy(c).wait_recv()
+            relay_copy(c).start()
 
     @pl.when(inner == 1)
     def _():
-        for k in range(panels):
-            own_copy(k, 1).wait_recv()
-            relay_copy(k).start()
+        for c in range(chunks):
+            own_copy(c).wait_recv()
+            relay_copy(c).start()
 
     for k in range(panels):
-        own_copy(k, 0).wait_recv()
-        relay_copy(k).wait_recv()
+        near_copy(k).wait_recv()
+    for c in range(chunks):
+        relay_copy(c).wait_recv()
 
     def tile_of(entry):
         right = entry // rows
@@ -347,47 +379,52 @@
 
     strip = 32
 
-    def gather(tiles, source):
-        wanted = [labels[source * capacity + r] for r in range(capacity)]
+    def gather(tiles, source, picks, target):
+        wanted = [labels[source * capacity + r] for r in picks]
         for c in range(width // strip):
             at = slice(c * strip, (c + 1) * strip)
-            parts = [tiles(r, at).astype(F32) for r in range(capacity)]
+            parts = [tiles(r, at).astype(F32) for r in picks]
 
             @pl.loop(0, slots)
             def _(q):
                 value = total[q, at]
-                for r in range(capacity):
-                    value += jnp.where(wanted[r] == q, parts[r], 0.0)
-                total[q, at] = value
-
-    gather(lambda r, at: packed[n_sub - 1, r, at], me)
-
-    @pl.loop(0, n_sub - 1)
+                for want, part in zip(wanted, parts):
+                    value += jnp.where(want == q, part, 0.0)
+                target[q, at] = value.astype(target.dtype)
+
+    every = range(capacity)
+    gather(lambda r, at: packed[n_sub - 1, r, at], me, every, total)
+
+    @pl.loop(0, n_sub - 2)
     def _(step):
         source = source_peer(step)
-        for r in range(capacity):
+        for r in every:
             out_copy(step, r, source, step).wait_recv()
-        gather(lambda r, at: incoming[step, r, at], source)
-
-    @pl.loop(0, slots)
-    def _(q):
-        result[q] = total[q].astype(BF16)
+        gather(lambda r, at: incoming[step, r, at], source, every, total)
+
+    final = n_sub - 2
+    source = source_peer(final)
+    for r in every:
+        out_copy(final, r, source, final).wait_recv()
+        target = result if r == capacity - 1 else total
+        gather(lambda r, at: incoming[final, r, at], source, [r], target)
 
     for k in range(panels):
-        own_copy(k, 0).wait_send()
-        relay_copy(k).wait_send()
+        near_copy(k).wait_send()
+    for c in range(chunks):
+        relay_copy(c).wait_send()
 
     @pl.when(inner == 0)
     def _():
-        for k in direct:
-            own_copy(k, 1).wait_send()
+        for c in direct:
+            own_copy(c).wait_send()
         for j in range(len(detoured)):
             detour_copy(j).wait_send()
 
     @pl.when(inner == 1)
     def _():
-        for k in range(panels):
-            own_copy(k, 1).wait_send()
+        for c in range(chunks):
+            own_copy(c).wait_send()
         for j in range(len(detoured)):
             forward_copy(j).wait_send()
 
@@ -416,11 +453,10 @@
     assert owner.shape[1] == n_tile * col_tiles
     capacity = (tile_count + n_sub - 1) // n_sub
     slots = base.shape[1]
-    room = (tile_count + 127) // 128 * 128
-    meta = (owner[0] * slots + slot[0]).T.reshape(1, tile_count)
-    meta = jnp.pad(meta, ((0, 0), (0, room - tile_count)))
+    meta = (owner[0] * slots + slot[0]).T
     dims = (n_sub, n_tile, panels, width, col_tiles, tile_count, capacity, slots)
-    relayed = panels * 3 // 8
+    chunks = panels * col_tiles
+    relayed = len(detour_chunks(chunks))
     any_spec = pl.BlockSpec(memory_space=pl.ANY)
     smem_spec = pl.BlockSpec(memory_space=pltpu.SMEM)
     dma = pltpu.SemaphoreType.DMA
@@ -428,7 +464,7 @@
         functools.partial(kernel, dims),
         out_shape=(
             jax.ShapeDtypeStruct((slots, width, width), BF16),
-            jax.ShapeDtypeStruct((n_sub, 1, room), jnp.int32),
+            jax.ShapeDtypeStruct((n_sub, *meta.shape), jnp.int32),
         ),
         in_specs=[smem_spec, any_spec, any_spec, any_spec, any_spec, any_spec],
         out_specs=(pl.BlockSpec(memory_space=pltpu.VMEM), any_spec),
@@ -437,19 +473,22 @@
             pltpu.VMEM(inverse.shape, F32),
             pltpu.VMEM(right_cols.shape, BF16),
             pltpu.VMEM((slots, width, width), BF16),
+            pltpu.VMEM((2, col_tiles, width, width), F32),
             pltpu.VMEM((n_tile * panels, col_tiles, width, width), BF16),
-            pltpu.VMEM((relayed, col_tiles, width, width), BF16),
+            pltpu.VMEM((relayed, width, width), BF16),
             pltpu.VMEM((n_sub, capacity, width, width), BF16),
             pltpu.VMEM((n_sub - 1, capacity, width, width), BF16),
             pltpu.VMEM((slots, width, width), F32),
             pltpu.SMEM((n_sub * capacity,), jnp.int32),
             pltpu.SMEM((n_sub * capacity,), jnp.int32),
-            pltpu.SMEM((n_sub, 1, room), jnp.int32),
+            pltpu.SMEM((n_sub, *meta.shape), jnp.int32),
             dma((6,)),
-            dma((2, panels)),
-            dma((2, panels)),
             dma((panels,)),
             dma((panels,)),
+            dma((chunks,)),
+            dma((chunks,)),
+            dma((chunks,)),
+            dma((chunks,)),
             dma((relayed,)),
             dma((relayed,)),
             dma((relayed,)),
@@ -461,7 +500,7 @@
             dma((3,)),
         ],
         compiler_params=pltpu.CompilerParams(
-            collective_id=0, has_side_effects=True, vmem_limit_bytes=62 * 1024 * 1024
+            collective_id=0, has_side_effects=True, vmem_limit_bytes=50 * 1024 * 1024
         ),
     )(meta, meta, lower_blocks, inverse, right_cols, base[0])
     return result[None]

time: 175 us -> 171 us (0.977)
  local copies, waits for them, and re-layouts: 3.7 us -> 1.33 us
    unnamed x2, local copies, waits for them, and re-layouts: 3.1 us -> 1.33 us
    pallas_call x1, Pallas kernels: 170 us -> 169 us  [shards(): pl.pallas_call(functools.partial(kernel, dims), out_shape=(jax.ShapeDtype...]
where the time goes in v2:
time: 171 us
  Pallas kernels  169 us (99%)
    pallas_call x1, Pallas kernels, shards(): pl.pallas_call(functools.partial(kernel, dims), out_shape=(jax.ShapeDtype...  169 us

profile of v2, /device:TPU:0, one launch (start us, length us, event | category | flops | bytes accessed | tf_op | source)
XLA Modules:
  0.0 170.8 jit_solution(7466736217492910970)
XLA Ops:
  0.0 0.7 multiply_add_fusion
  0.7 168.7 %shard_map.64 = (bf16[16,256,256]{2,1,0:T(8,128)(2,1)S(1)}, s32[8,3,12]{2,1,0:T(4,128)}) custom-call(s32[3,12]{1,0:T(4,128)S(1)} %bitcast.11, s32[3,12]{1,0:T(4,128)S(1)} %bitcast.12, bf16[28,256,256]{2,1,0:T(8,128)(2,1)} %bitcast.13, f32[8,256,256]{2,1,0:T(8,128)} %bitcast.15, bf16[8,256,768]{2,1,0:T(8,128)(2,1)} %bitcast.14, bf16[16,256,256]{2,1,0:T(8,128)(2,1)} %bitcast.16), custom_call_target="tpu_custom_call" | custom-call | tf_op jit(solution)/shard_map/pallas_call | solution.py:463
  169.5 1.3 copy.11
  (1 shorter events, 0.0 us)
